TPU v7x, 32 devices: a whole 2x2x4 slice. The times are simulated.
32 devices in a mesh: view: 4 (over x, core), depth: 8 (over z, y).
Axes of the slice: x: 2, y: 2, z: 4, core: 2. Of those that a mesh axis runs over, the one named last changes fastest.
Arguments:
- volume: float32 [128, 128, 512], P(('view', 'depth')), may hold values from -6 to 6
- step_weights: float32 [4, 8, 64], P('view'), may hold values from -0.75 to 0.75
- row_interp: float32 [4, 64, 64], P('view'), may hold values from -0.75 to 0.75
- col_interp: float32 [4, 64, 64], P('view'), may hold values from -0.75 to 0.75
- tf_table: float32 [8, 8], replicated, may hold values from -3 to 3
- materials: int32 [2, 2, 8], P(None, None, 'depth'), may hold values from 0 to 7
- entry: int32 [4, 128, 128], P('view'), may hold values from 0 to 3
Outputs:
- picture: float32 [4, 3, 128, 128], P('view', None, 'depth')
All inputs are finite; a program needn't handle non-finite values.
Results may differ from a plain program's by a relative error of at most 0.00018.
Values sent between devices are 32-bit elements; how exact they have to be, the bound alone decides.
No kernel may reach another device: no remote copies, remote signals or barrier semaphores. Data moves between devices by JAX's collectives and lax.ppermute only.
A program may use at most 64 MiB of HBM per device.

v0:
```python
import jax
import jax.numpy as jnp
from jax import lax
from jax.sharding import PartitionSpec as P


def prefix(part, axis, combine, identity):
    place = lax.axis_index(axis)
    gathered = lax.all_gather(part, axis)
    state = jnp.zeros_like(part) + jnp.asarray(identity, part.dtype)

    def one(lap, state):
        return combine(state, lax.dynamic_index_in_dim(gathered, lap, 0, False))

    return lax.fori_loop(0, place, one, state)


def finish_brick(first, rows_map, cols_map):
    highest = lax.Precision.HIGHEST
    edge = rows_map.shape[0]
    count_steps, total_rows, total_cols = first.shape
    second = first.reshape(count_steps, total_rows // edge, edge, total_cols)
    second = jnp.einsum("stky,rk->stry", second, rows_map, precision=highest)
    third = second.reshape(count_steps, total_rows, total_cols // edge, edge)
    third = jnp.einsum("szuj,cj->szuc", third, cols_map, precision=highest)
    return third.reshape(count_steps, total_rows, total_cols)


def expand_classes(classes, tf_table, edge):
    choices_range = jnp.arange(tf_table.shape[0], dtype=jnp.int32)
    onehot = (classes[:, :, None] == choices_range).astype(jnp.float32)
    tiles = jnp.einsum("abm,mc->cab", onehot, tf_table, precision=lax.Precision.HIGHEST)
    count_coef, tiles_rows, tiles_cols = tiles.shape
    spread = jnp.broadcast_to(
        tiles[:, :, None, :, None], (count_coef, tiles_rows, edge, tiles_cols, edge)
    )
    return spread.reshape(count_coef, tiles_rows * edge, tiles_cols * edge)


def shade(samples, coefficients, live_mask, step_length):
    emission = jax.nn.softplus(coefficients[0:3, None] * samples[None] + coefficients[3:6, None])
    tau = (
        step_length
        * live_mask[None]
        * jax.nn.softplus(coefficients[6][None] * samples + coefficients[7][None])
    )
    earlier = jnp.cumsum(tau, axis=0) - tau
    weights = jnp.exp(-earlier) * (1.0 - jnp.exp(-tau))
    colours = jnp.sum(weights[None] * emission, axis=1)
    passed = jnp.exp(-jnp.sum(tau, axis=0))
    return (colours, passed)


def multiply(earlier, later):
    return earlier * later


def shards(volume, step_weights, row_interp, col_interp, tf_table, materials, entry):
    view_count = lax.axis_size("view")
    depth_count = lax.axis_size("depth")
    depth_index = lax.axis_index("depth")
    planes, lateral, span_cells = volume.shape
    brick_edge = span_cells // depth_count
    all_weights = lax.all_gather(step_weights, "view", axis=0, tiled=True)
    count_steps = all_weights.shape[1]
    cells = volume.reshape(planes, lateral, depth_count, brick_edge)
    contracted = jnp.einsum("zybi,gsi->gbszy", cells, all_weights, precision=lax.Precision.HIGHEST)
    contracted = contracted.reshape(view_count * depth_count, count_steps, planes, lateral)
    received = lax.all_to_all(
        contracted, ("view", "depth"), split_axis=0, concat_axis=2, tiled=True
    )
    samples = finish_brick(received[0], row_interp[0], col_interp[0])
    coefficients = expand_classes(materials[:, :, 0], tf_table, brick_edge)
    live_mask = (entry[0] <= depth_index).astype(jnp.float32)
    step_length = 2.0 / (samples.shape[0] * depth_count)
    colours, passed = shade(samples, coefficients, live_mask, step_length)
    before = prefix(passed, "depth", multiply, jnp.ones_like(passed))
    terms = before[None] * colours
    rows_part = lax.psum_scatter(terms, "depth", scatter_dimension=1, tiled=True)
    return rows_part[None]


def solution(mesh):
    placed = (
        P(("view", "depth"), None, None),
        P("view", None, None),
        P("view", None, None),
        P("view", None, None),
        P(),
        P(None, None, "depth"),
        P("view", None, None),
    )
    return jax.shard_map(
        shards,
        mesh=mesh,
        in_specs=placed,
        out_specs=P("view", None, "depth", None),
        check_vma=False,
    )
```

profile of v0, /device:TPU:0, one launch (start us, length us, event | category | flops | bytes accessed | tf_op | source)
XLA Modules:
  0.0 142.9 jit_solution(2641212617554178664)
XLA Ops:
  6.5 6.5 %all_gather.7 = f32[4,8,64]{2,1,0:T(8,128)S(1)} all-gather(f32[1,8,64]{2,1,0:T(8,128)} %param.10), channel_id=1, replica_groups=mesh['view'=4,'depth'=8] {'view'}, dimensions={0}, use_global_device_ids=true | all-gather | bytes 10240 | tf_op jit(solution)/shard_map/all_gather | solution.py:64
  13.0 1.5 %copy.50 = f32[4,128,512]{1,2,0:T(8,128)S(1)} copy(f32[4,128,512]{2,1,0:T(8,128)} %param.9) | data formatting | bytes 2097152 | tf_op args[0]
  14.6 0.6 convolution_bitcast_fusion.1
  15.3 0.9 copy.51
  16.1 6.3 %all-to-all-start = ((f32[32,8,4,128]{3,1,2,0:T(8,128)}), f32[32,8,4,128]{3,1,2,0:T(8,128)S(1)}, u32[]{:S(2)}, u32[]{:S(2)}) async-start(f32[32,8,4,128]{3,1,2,0:T(8,128)} %bitcast.10), calls=%async_computation | async-start | bytes 1048576 | tf_op jit(solution)/shard_map/all_to_all | solution.py:69
  22.5 0.2 convolution_bitcast_fusion.2
  22.8 0.1 copy.59
  22.9 0.1 copy.65
  23.0 0.1 copy.66
  23.4 0.1 copy.61
  23.6 0.1 copy.48
  23.7 0.1 broadcast_in_dim.41
  23.8 0.1 broadcast_in_dim.42
  23.9 0.1 broadcast_in_dim.43
  24.0 0.1 broadcast_in_dim.44
  24.1 0.2 broadcast_in_dim.46
  24.3 0.2 add.65
  24.5 0.2 broadcast_in_dim.45
  24.7 0.2 mul.110
  25.0 13.6 %all-to-all-done = f32[32,8,4,128]{3,1,2,0:T(8,128)S(1)} async-done(((f32[32,8,4,128]{3,1,2,0:T(8,128)}), f32[32,8,4,128]{3,1,2,0:T(8,128)S(1)}, u32[]{:S(2)}, u32[]{:S(2)}) %all-to-all-start) | async-done | bytes 524320 | tf_op jit(solution)/shard_map/all_to_all | solution.py:69
  38.6 0.1 copy.52
  38.8 0.6 convolution_bitcast_fusion
  39.4 0.6 reshape.101
  40.0 1.3 fusion.21
  41.4 0.4 multiply_reduce_fusion
  41.9 0.2 copy.60
  42.1 0.5 fusion.4
  42.6 0.2 copy.58
  42.8 31.4 %all_gather.8 = f32[8,128,128]{2,1,0:T(8,128)S(1)} all-gather(f32[1,128,128]{2,1,0:T(8,128)S(1)} %copy.55), channel_id=1, replica_groups=mesh['view'=4,'depth'=8] {'depth'}, dimensions={0}, use_global_device_ids=true | all-gather | bytes 589824 | tf_op jit(solution)/shard_map/all_gather | solution.py:9
  74.2 1.0 fusion.1
  75.2 0.7 broadcast_multiply_fusion
  75.9 60.1 %reduce-scatter.2.cloned.1.call-done = f32[3,16,128]{2,1,0:T(8,128)} async-done(((f32[3,128,128]{2,1,0:T(8,128)}), f32[3,16,128]{2,1,0:T(8,128)}) %reduce-scatter.2.cloned.1.call-update) | async-done | bytes 24592 | tf_op jit(solution)/shard_map/reduce_scatter | solution.py:79
  (24 shorter events, 0.7 us)
Async XLA Ops:
  6.5 33.5 %copy-start = (f32[1,64,64]{2,1,0:T(8,128)S(1)}, f32[1,64,64]{2,1,0:T(8,128)}, u32[]{:S(2)}) copy-start(f32[1,64,64]{2,1,0:T(8,128)} %param.12) | copy-start | bytes 49156
  15.2 7.2 %copy-start.3 = (f32[8,8]{1,0:T(8,128)S(1)}, f32[8,8]{1,0:T(8,128)}, u32[]{:S(2)}) copy-start(f32[8,8]{1,0:T(8,128)} %param.13) | copy-start | bytes 772
  15.2 7.2 %copy-start.4 = (s32[2,2,1]{1,2,0:T(1,128)S(1)}, s32[2,2,1]{1,2,0:T(1,128)}, u32[]{:S(2)}) copy-start(s32[2,2,1]{1,2,0:T(1,128)} %param.14) | copy-start | bytes 52
  15.2 8.3 %copy-start.1 = (s32[1,128,128]{2,1,0:T(8,128)S(1)}, s32[1,128,128]{2,1,0:T(8,128)}, u32[]{:S(2)}) copy-start(s32[1,128,128]{2,1,0:T(8,128)} %param.15) | copy-start | bytes 196612
  16.1 22.5 %all-to-all-start = ((f32[32,8,4,128]{3,1,2,0:T(8,128)}), f32[32,8,4,128]{3,1,2,0:T(8,128)S(1)}, u32[]{:S(2)}, u32[]{:S(2)}) async-start(f32[32,8,4,128]{3,1,2,0:T(8,128)} %bitcast.10), calls=%async_computation | async-start | bytes 1048576 | tf_op jit(solution)/shard_map/all_to_all | solution.py:69
  22.4 113.6 %reduce-scatter.2.cloned.1.call-start = ((), (), s32[]{:S(2)}) async-start(), calls=%async_computation.2 | async-start | bytes 221184 | tf_op jit(solution)/shard_map/reduce_scatter | solution.py:79
  24.7 14.1 %copy-start.2 = (f32[1,64,64]{2,1,0:T(8,128)S(1)}, f32[1,64,64]{2,1,0:T(8,128)}, u32[]{:S(2)}) copy-start(f32[1,64,64]{2,1,0:T(8,128)} %param.11) | copy-start | bytes 49156
Sparse Core Ops, SparseCore 0:
  76.0 59.9 reduce-scatter.1
where the time goes:
time: 143 us
  waiting for transfers between devices  73.8 us (52%)
  blocking collectives  37.9 us (27%)
  between operations  13.6 us (10%)
  starting transfers between devices  6.33 us (4%)
  local copies, waits for them, and re-layouts  5.89 us (4%)
  matrix products  2.78 us (2%)
  other arithmetic  2.59 us (2%)
    reduce_scatter x1, waiting for transfers between devices, shards(): lax.psum_scatter(terms, 'depth', scatter_dimension=1, tiled=True)  60.1 us
    all_gather x1, blocking collectives, prefix(): gathered = lax.all_gather(part, axis)  31.4 us
    all_to_all x1, waiting for transfers between devices, shards(): lax.all_to_all(contracted, ('view', 'depth'), split_axis=0, concat_axis=2...  13.6 us
    all_gather x1, blocking collectives, shards(): all_weights = lax.all_gather(step_weights, 'view', axis=0, tiled=True)  6.49 us
    all_to_all x1, starting transfers between devices, shards(): lax.all_to_all(contracted, ('view', 'depth'), split_axis=0, concat_axis=2...  6.29 us
  transfers between devices with their start and end apart: 2, of which 2 were waited for; matrix products, arithmetic and copies ran while one was open for 2% of the time, Pallas kernels for 0%

commit v1 on v0

v1 whole, which is shorter than its diff:
```python
import functools

import jax
import jax.numpy as jnp
from jax import lax
from jax.experimental import pallas as pl
from jax.experimental.pallas import tpu as pltpu
from jax.sharding import PartitionSpec as P

LANES = 128
SUB = 8
COEF = 8
HIGHEST = lax.Precision.HIGHEST
NT = (((1,), (1,)), ((), ()))
NN = (((1,), (0,)), ((), ()))


def split(x):
    hi = x.astype(jnp.bfloat16)
    return hi, (x - hi.astype(jnp.float32)).astype(jnp.bfloat16)


def dot3(a, b, dims):
    dot = functools.partial(
        lax.dot_general, dimension_numbers=dims, preferred_element_type=jnp.float32
    )
    return dot(a[0], b[0]) + (dot(a[0], b[1]) + dot(a[1], b[0]))


def softplus(v):
    e = jnp.exp(-jnp.abs(v))
    small = e * (1.0 - 0.5 * e)
    return jnp.maximum(v, 0.0) + jnp.where(e < 1e-4, small, jnp.log(1.0 + e))


def send_kernel(depth, vol_ref, steps_ref, cols_ref, classes_ref, table_ref, out_ref):
    planes, lateral, span = vol_ref.shape
    views, steps, edge = steps_ref.shape
    bricks = span // edge
    tiles_z, tiles_y = classes_ref.shape[:2]
    per = lateral // depth

    weights = steps_ref[...].reshape(views * steps, edge)
    tiled = jnp.concatenate([weights] * bricks, axis=1)
    lane = lax.broadcasted_iota(jnp.int32, (bricks, span), 1)
    brick = lax.broadcasted_iota(jnp.int32, (bricks, span), 0)
    own = lane // edge == brick
    ray = jnp.where(own[None], tiled[:, None, :], 0.0).reshape(views * steps * bricks, span)
    cells = vol_ref[...].reshape(planes * lateral, span)
    first = dot3(split(cells), split(ray), NT)
    first_hi, first_lo = split(first)

    half = lax.broadcasted_iota(jnp.int32, (SUB, LANES), 1) < LANES // 2
    zero = jnp.zeros((edge, edge), jnp.float32)
    for pair in range(views // 2):
        rows = []
        for view in (2 * pair, 2 * pair + 1):
            c = cols_ref[view]
            for tile in range(tiles_y):
                rows.append(jnp.concatenate([c if t == tile else zero for t in range(tiles_y)], axis=1))
        maps = split(jnp.concatenate(rows, axis=0))
        for plane in range(planes):
            at = slice(plane * lateral, (plane + 1) * lateral)
            to = slice(pair * LANES, (pair + 1) * LANES)
            second = dot3(maps, (first_hi[at, to], first_lo[at, to]), NN)
            for k in range(2):
                for d in range(depth):
                    base = k * lateral + d * per
                    a = second[base : base + SUB]
                    b = second[base + SUB : base + 2 * SUB]
                    if k == 0:
                        b = pltpu.roll(b, LANES // 2, 1)
                    else:
                        a = pltpu.roll(a, LANES // 2, 1)
                    block = jnp.where(half, a, b)
                    out_ref[(2 * pair + k) * depth + d, plane * SUB : (plane + 1) * SUB, 0, :] = block

    lane = lax.broadcasted_iota(jnp.int32, (1, LANES), 1)
    for u in range(tiles_y):
        row = jnp.zeros((1, LANES), jnp.float32)
        for t in range(tiles_z):
            for ch in range(COEF):
                row = jnp.where(lane == t * COEF + ch, table_ref[classes_ref[t, u, 0], ch], row)
        for v in range(views):
            for d in range(depth):
                if d * per // edge == u:
                    out_ref[v * depth + d, planes * SUB : planes * SUB + 1, 0, :] = row


def render_kernel(step_length, recv_ref, maps_ref, entry_ref, out_ref, cells):
    sources, rows_block = recv_ref.shape[:2]
    data = rows_block - 1
    columns, rows = entry_ref.shape
    bricks = steps = SUB
    for s in range(sources):
        cells[s * data : (s + 1) * data, :] = recv_ref[s, 0:data, 0, :]
    maps = split(maps_ref[...])

    packed = jnp.concatenate([recv_ref[b, data : data + 1, 0, :] for b in range(bricks)], axis=0)
    lane = lax.broadcasted_iota(jnp.int32, (bricks, rows), 1)
    upper = lane >= rows // 2
    coef = []
    for ch in range(COEF):
        low = jnp.broadcast_to(packed[:, ch : ch + 1], (bricks, rows))
        high = jnp.broadcast_to(packed[:, COEF + ch : COEF + ch + 1], (bricks, rows))
        coef.append(jnp.where(upper, high, low))
    brick = lax.broadcasted_iota(jnp.int32, (bricks, rows), 0)

    shown = [[None] * columns for _ in range(3)]
    for x in range(SUB):
        planes = cells[pl.ds(x, rows, stride=SUB), :]
        samples = dot3(split(planes.T), maps, NN)
        for low in range(2):
            c = low * SUB + x
            live = jnp.where(entry_ref[c : c + 1, :] <= brick, step_length, 0.0)
            total = jnp.zeros((bricks, rows), jnp.float32)
            before = jnp.ones((bricks, rows), jnp.float32)
            colours = [jnp.zeros((bricks, rows), jnp.float32) for _ in range(3)]
            for s in range(steps):
                at = (low * steps + s) * bricks
                v = samples[at : at + bricks]
                total = total + live * softplus(coef[6] * v + coef[7])
                after = jnp.exp(-total)
                weight = before - after
                before = after
                for ch in range(3):
                    colours[ch] = colours[ch] + weight * softplus(coef[ch] * v + coef[3 + ch])
            front = total
            for shift in (1, 2, 4):
                front = front + jnp.where(brick >= shift, pltpu.roll(front, shift, 0), 0.0)
            reach = jnp.exp(total - front)
            for ch in range(3):
                shown[ch][c] = jnp.sum(reach * colours[ch], axis=0, keepdims=True)
    blank = jnp.zeros((LANES - 3 * columns, rows), jnp.float32)
    image = jnp.concatenate([r for ch in shown for r in ch] + [blank], axis=0)
    out_ref[...] = image.T.reshape(out_ref.shape)


def unpack_kernel(columns, recv_ref, out_ref):
    sources, rows, _ = recv_ref.shape
    owner = lax.broadcasted_iota(jnp.int32, (rows, LANES), 1) // columns
    for ch in range(3):
        out = jnp.zeros((rows, LANES), jnp.float32)
        for s in range(sources):
            moved = pltpu.roll(recv_ref[s], ((s - ch) * columns) % LANES, 1)
            out = jnp.where(owner == s, moved, out)
        out_ref[0, ch] = out


def vmem():
    return pl.BlockSpec(memory_space=pltpu.VMEM)


def smem():
    return pl.BlockSpec(memory_space=pltpu.SMEM)


def with_kernels(volume, all_steps, all_cols, row_interp, tf_table, materials, entry):
    views, steps, edge = all_steps.shape
    depth = lax.axis_size("depth")
    planes, lateral, span = volume.shape
    devices = views * depth
    per = lateral // depth
    rows = devices * planes
    step_length = 2.0 / (steps * depth)
    blocks = pl.pallas_call(
        functools.partial(send_kernel, depth),
        out_shape=jax.ShapeDtypeStruct((devices, planes * SUB + 1, 1, LANES), jnp.float32),
        in_specs=[vmem(), vmem(), vmem(), smem(), smem()],
        out_specs=vmem(),
        name="send",
    )(volume, all_steps, all_cols, materials, tf_table)
    recv = lax.all_to_all(blocks, ("view", "depth"), split_axis=0, concat_axis=0, tiled=True)

    maps = jnp.kron(jnp.eye(rows // edge, dtype=jnp.float32), row_interp[0].T)
    entry_own = lax.dynamic_slice_in_dim(entry[0].T, lax.axis_index("depth") * per, per, 0)
    image = pl.pallas_call(
        functools.partial(render_kernel, step_length),
        out_shape=jax.ShapeDtypeStruct((depth, rows // depth, LANES), jnp.float32),
        in_specs=[vmem()] * 3,
        out_specs=vmem(),
        scratch_shapes=[pltpu.VMEM((devices * planes * SUB, LANES), jnp.float32)],
        name="render",
    )(recv, maps, entry_own)
    turned = lax.all_to_all(image, "depth", split_axis=0, concat_axis=0, tiled=True)
    return pl.pallas_call(
        functools.partial(unpack_kernel, per),
        out_shape=jax.ShapeDtypeStruct((1, 3, rows // depth, lateral), jnp.float32),
        in_specs=[vmem()],
        out_specs=vmem(),
        name="unpack",
    )(turned)


def with_arrays(volume, all_steps, all_cols, row_interp, tf_table, materials, entry):
    views, steps, edge = all_steps.shape
    depth = lax.axis_size("depth")
    planes, lateral, span = volume.shape
    devices = views * depth
    per = lateral // depth
    rows = devices * planes
    tiles_z, tiles_y = materials.shape[:2]
    step_length = 2.0 / (steps * depth)
    cells = volume.reshape(planes, tiles_y, edge, depth, edge)
    first = jnp.einsum("pujbi,vsi->vpujbs", cells, all_steps, precision=HIGHEST)
    second = jnp.einsum("vpujbs,vcj->vpucbs", first, all_cols, precision=HIGHEST)
    second = second.reshape(views, planes, depth, per, depth, steps).transpose(0, 2, 1, 3, 4, 5)
    second = second.reshape(devices, planes * per * depth * steps)
    own = tf_table[materials[:, :, 0]].transpose(1, 0, 2).reshape(tiles_y, tiles_z * COEF)
    own = jnp.tile(jnp.repeat(own, edge // per, axis=0), (views, 1))
    payload = jnp.concatenate([second, own], axis=1)
    payload = jnp.pad(payload, ((0, 0), (0, -payload.shape[1] % LANES)))
    payload = payload.reshape(devices, -1, 1, LANES)
    recv = lax.all_to_all(payload, ("view", "depth"), split_axis=0, concat_axis=0, tiled=True)
    recv = recv.reshape(devices, -1)
    size = second.shape[1]
    coef = recv[:depth, size : size + tiles_z * COEF].reshape(depth, tiles_z, COEF)
    coef = jnp.repeat(coef.transpose(2, 1, 0), edge, axis=1)[:, :, None, :, None]
    third = recv[:, :size].reshape(tiles_z, edge, per, depth, steps)
    third = jnp.einsum("tkcbs,rk->trcbs", third, row_interp[0], precision=HIGHEST)
    samples = third.reshape(rows, per, depth, steps)
    entry_own = lax.dynamic_slice_in_dim(entry[0], lax.axis_index("depth") * per, per, 1)
    live = (entry_own[:, :, None] <= jnp.arange(depth)).astype(jnp.float32)
    tau = step_length * live[..., None] * jax.nn.softplus(coef[6] * samples + coef[7])
    flat = tau.reshape(rows, per, depth * steps)
    earlier = (jnp.cumsum(flat, axis=2) - flat).reshape(tau.shape)
    weights = jnp.exp(-earlier) * (1.0 - jnp.exp(-tau))
    emission = jax.nn.softplus(coef[0:3] * samples + coef[3:6])
    image = jnp.sum(weights * emission, axis=(3, 4))
    turned = lax.all_to_all(image, "depth", split_axis=1, concat_axis=2, tiled=True)
    return turned[None]


def shards(volume, step_weights, row_interp, col_interp, tf_table, materials, entry):
    views = lax.axis_size("view")
    depth = lax.axis_size("depth")
    all_steps = lax.all_gather(step_weights, "view", axis=0, tiled=True)
    all_cols = lax.all_gather(col_interp, "view", axis=0, tiled=True)
    planes, lateral, span = volume.shape
    steps, edge = step_weights.shape[1:]
    rows = views * depth * planes
    fits = (
        depth == SUB
        and steps == SUB
        and edge == LANES // 2
        and lateral == LANES
        and rows == LANES
        and views % 2 == 0
        and span == depth * edge
    )
    run = with_kernels if fits else with_arrays
    return run(volume, all_steps, all_cols, row_interp, tf_table, materials, entry)


def solution(mesh):
    placed = (
        P(("view", "depth"), None, None),
        P("view", None, None),
        P("view", None, None),
        P("view", None, None),
        P(),
        P(None, None, "depth"),
        P("view", None, None),
    )
    return jax.shard_map(
        shards,
        mesh=mesh,
        in_specs=placed,
        out_specs=P("view", None, "depth", None),
        check_vma=False,
    )
```

time: 143 us -> 58.9 us (0.41)
  waiting for transfers between devices: 73.8 us -> 14.9 us
  between operations: 13.6 us -> 0.05 us
  blocking collectives: 37.9 us -> 25.3 us
  Pallas kernels: 0 us -> 9.28 us
  local copies, waits for them, and re-layouts: 5.89 us -> 3.06 us
  matrix products: 2.78 us -> 0 us
  other arithmetic: 2.59 us -> 0.11 us
    reduce_scatter x1 -> x0, waiting for transfers between devices: 60.1 us -> none  [shards(): lax.psum_scatter(terms, 'depth', scatter_dimension=1, tiled=True)]
    all_gather x2, blocking collectives: 37.9 us -> 14.5 us  [the longest x1 8.17 us: shards(): all_steps = lax.all_gather(step_weights, 'view', axis=0, tiled=True)]
    all_to_all x0 -> x1, blocking collectives: none -> 10.9 us  [with_kernels(): lax.all_to_all(image, 'depth', split_axis=0, concat_axis=0, tiled=True)]
    pallas_call x0 -> x3, Pallas kernels: none -> 9.28 us  [the longest x1 4.05 us: with_kernels(): pl.pallas_call(functools.partial(send_kernel, depth), out_shape=jax.Shape...]
    dot_general x4 -> x0, matrix products: 2.78 us -> none  [the longest x1 1.33 us: finish_brick(): third = jnp.einsum('szuj,cj->szuc', third, cols_map, precision=highest)]
  transfers between devices with their start and end apart: 2 -> 1, of which waited for: 2 -> 1; matrix products, arithmetic and copies ran while one was open for 2% -> 3% of each run, Pallas kernels for 0% -> 0%
where the time goes in v1:
time: 58.9 us; the launch traced here: 58.3 us
  blocking collectives  25.3 us (43%)
  waiting for transfers between devices  14.9 us (25%)
  Pallas kernels  9.28 us (16%)
  starting transfers between devices  5.63 us (10%)
  local copies, waits for them, and re-layouts  3.06 us (5%)
    all_to_all x1, waiting for transfers between devices, with_kernels(): lax.all_to_all(blocks, ('view', 'depth'), split_axis=0, concat_axis=0, ti...  14.9 us
    all_to_all x1, blocking collectives, with_kernels(): lax.all_to_all(image, 'depth', split_axis=0, concat_axis=0, tiled=True)  10.9 us
    all_gather x1, blocking collectives, shards(): all_steps = lax.all_gather(step_weights, 'view', axis=0, tiled=True)  8.17 us
    all_gather x1, blocking collectives, shards(): all_cols = lax.all_gather(col_interp, 'view', axis=0, tiled=True)  6.28 us
    all_to_all x1, starting transfers between devices, with_kernels(): lax.all_to_all(blocks, ('view', 'depth'), split_axis=0, concat_axis=0, ti...  5.63 us
    pallas_call x1, Pallas kernels, with_kernels(): pl.pallas_call(functools.partial(send_kernel, depth), out_shape=jax.Shape...  4.05 us
    pallas_call x1, Pallas kernels, with_kernels(): pl.pallas_call(functools.partial(render_kernel, step_length), out_shape=j...  3.67 us
    pallas_call x1, Pallas kernels, with_kernels(): pl.pallas_call(functools.partial(unpack_kernel, per), out_shape=jax.Shape...  1.56 us
  transfers between devices with their start and end apart: 1, of which 1 were waited for; matrix products, arithmetic and copies ran while one was open for 3% of the time, Pallas kernels for 0%

profile of v1, /device:TPU:0, one launch (start us, length us, event | category | flops | bytes accessed | tf_op | source)
XLA Modules:
  0.0 58.3 jit_solution(10105031112866584523)
XLA Ops:
  0.0 0.0 copy-start
  0.0 8.2 %all_gather.6.steps_ref = f32[4,8,64]{2,1,0:T(8,128)} all-gather(f32[1,8,64]{2,1,0:T(8,128)} %param.8), channel_id=1, replica_groups=mesh['view'=4,'depth'=8] {'view'}, dimensions={0}, use_global_device_ids=true | all-gather | bytes 10240 | tf_op jit(solution)/shard_map/all_gather | solution.py:237
  8.2 0.0 copy-start.3
  8.2 6.3 %all_gather.7.cols_ref = f32[4,64,64]{2,1,0:T(8,128)} all-gather(f32[1,64,64]{2,1,0:T(8,128)} %param.10), channel_id=1, replica_groups=mesh['view'=4,'depth'=8] {'view'}, dimensions={0}, use_global_device_ids=true | all-gather | bytes 81920 | tf_op jit(solution)/shard_map/all_gather | solution.py:238
  14.5 0.0 copy-done.3
  14.5 0.7 %copy.11.classes_ref = s32[2,2,1]{2,1,0:T(2,128)} copy(s32[2,2,1]{1,2,0:T(1,128)S(1)} %copy-done.3) | data formatting | bytes 32 | tf_op args[5]
  15.1 4.0 %send.1 = f32[32,33,1,128]{3,2,1,0:T(1,128)} custom-call(f32[4,128,512]{2,1,0:T(8,128)} %vol_ref.1, f32[4,8,64]{2,1,0:T(8,128)} %all_gather.6.steps_ref, f32[4,64,64]{2,1,0:T(8,128)} %all_gather.7.cols_ref, s32[2,2,1]{2,1,0:T(2,128)} %copy.11.classes_ref, f32[8,8]{1,0:T(8,128)} %table_ref.1), custom_call_target="tpu_custom_call" | custom-call | tf_op jit(solution)/shard_map/send/pallas_call | solution.py:166
  19.2 0.0 copy-start.2
  19.2 5.6 %all-to-all-start = ((f32[32,33,1,128]{3,2,1,0:T(1,128)}), f32[32,33,1,128]{3,2,1,0:T(1,128)S(1)}, u32[]{:S(2)}, u32[]{:S(2)}) async-start(f32[32,33,1,128]{3,2,1,0:T(1,128)} %send.1), calls=%async_computation | async-start | bytes 1081344 | tf_op jit(solution)/shard_map/all_to_all | solution.py:173
  24.8 0.0 copy-done.2
  24.8 0.1 copy.12
  24.9 0.1 broadcast_multiply_fusion
  25.0 0.8 %mul.30.maps_ref = f32[128,128]{1,0:T(8,128)} reshape(f32[2,64,2,64]{3,2,1,0:T(2,128)S(1)} %broadcast_multiply_fusion) | data formatting | bytes 131072 | tf_op jit(solution)/shard_map/jit(kron)/mul | solution.py:175
  25.8 0.0 copy-done
  25.8 0.1 constant_dynamic-slice_fusion
  25.9 0.7 %copy.13 = s32[1,128,16]{1,2,0:T(8,128)} copy(s32[1,128,16]{2,1,0:T(8,128)S(1)} %constant_dynamic-slice_fusion) | data formatting | bytes 16384 | tf_op jit(solution)/shard_map/dynamic-slice.1
  26.6 14.9 %all-to-all-done.recv_ref = f32[32,33,1,128]{3,2,1,0:T(1,128)S(1)} async-done(((f32[32,33,1,128]{3,2,1,0:T(1,128)}), f32[32,33,1,128]{3,2,1,0:T(1,128)S(1)}, u32[]{:S(2)}, u32[]{:S(2)}) %all-to-all-start) | async-done | bytes 540704 | tf_op jit(solution)/shard_map/all_to_all | solution.py:173
  41.4 0.0 copy-start.1
  41.4 0.8 %copy-done.1 = f32[32,33,1,128]{3,2,1,0:T(1,128)} copy-done((f32[32,33,1,128]{3,2,1,0:T(1,128)}, f32[32,33,1,128]{3,2,1,0:T(1,128)S(1)}, u32[]{:S(2)}) %copy-start.1) | copy-done | bytes 540696
  42.2 3.7 %render.1 = f32[8,16,128]{2,1,0:T(8,128)} custom-call(f32[32,33,1,128]{3,2,1,0:T(1,128)} %copy-done.1, f32[128,128]{1,0:T(8,128)} %mul.30.maps_ref, s32[16,128]{1,0:T(8,128)} %bitcast.6), custom_call_target="tpu_custom_call" | custom-call | tf_op jit(solution)/shard_map/render/pallas_call | solution.py:177
  45.9 10.9 %all_to_all.10.recv_ref = f32[8,16,128]{2,1,0:T(8,128)} all-to-all(f32[8,16,128]{2,1,0:T(8,128)} %render.1), channel_id=1, replica_groups=mesh['view'=4,'depth'=8] {'depth'}, dimensions={0} | all-to-all | bytes 131072 | tf_op jit(solution)/shard_map/all_to_all | solution.py:185
  56.7 1.6 %unpack.1 = f32[1,3,16,128]{3,2,1,0:T(8,128)} custom-call(f32[8,16,128]{2,1,0:T(8,128)} %all_to_all.10.recv_ref), custom_call_target="tpu_custom_call" | custom-call | tf_op jit(solution)/shard_map/unpack/pallas_call | solution.py:186
  (1 shorter events, 0.0 us)
Async XLA Ops:
  0.0 25.8 %copy-start = (s32[1,128,128]{2,1,0:T(8,128)S(1)}, s32[1,128,128]{2,1,0:T(8,128)}, u32[]{:S(2)}) copy-start(s32[1,128,128]{2,1,0:T(8,128)} %param.13) | copy-start | bytes 196612
  8.2 6.3 %copy-start.3 = (s32[2,2,1]{1,2,0:T(1,128)S(1)}, s32[2,2,1]{1,2,0:T(1,128)}, u32[]{:S(2)}) copy-start(s32[2,2,1]{1,2,0:T(1,128)} %param.12) | copy-start | bytes 52
  19.2 5.6 %copy-start.2 = (f32[1,64,64]{2,1,0:T(8,128)S(1)}, f32[1,64,64]{2,1,0:T(8,128)}, u32[]{:S(2)}) copy-start(f32[1,64,64]{2,1,0:T(8,128)} %param.9) | copy-start | bytes 49156
  19.2 22.2 %all-to-all-start = ((f32[32,33,1,128]{3,2,1,0:T(1,128)}), f32[32,33,1,128]{3,2,1,0:T(1,128)S(1)}, u32[]{:S(2)}, u32[]{:S(2)}) async-start(f32[32,33,1,128]{3,2,1,0:T(1,128)} %send.1), calls=%async_computation | async-start | bytes 1081344 | tf_op jit(solution)/shard_map/all_to_all | solution.py:173
  41.4 0.8 %copy-start.1 = (f32[32,33,1,128]{3,2,1,0:T(1,128)}, f32[32,33,1,128]{3,2,1,0:T(1,128)S(1)}, u32[]{:S(2)}) copy-start(f32[32,33,1,128]{3,2,1,0:T(1,128)S(1)} %all-to-all-done.recv_ref) | copy-start | bytes 1622020
